TPU v7x, 32 devices: a whole 2x2x4 slice. The times are simulated.
32 devices in a mesh: sfc: 8 (over z, x), grp: 4 (over y, core).
Axes of the slice: x: 2, y: 2, z: 4, core: 2. Of those that a mesh axis runs over, the one named last changes fastest.
Arguments:
- source: float32 [32, 16, 1024], P('sfc', None, 'grp'), may hold values from -8 to 8
- layer_counts: int32 [8], P('sfc'), may hold values from 1 to 4, 21 in all
Outputs:
- solution: float32 [32, 16, 1024], P('sfc', None, 'grp')
- residual: float32 [32, 16, 1024], P('sfc', None, 'grp')
- direction: float32 [32, 16, 1024], P('sfc', None, 'grp')
Inputs may be any that keep to these rules, and one draw needn't show every extreme that they name: `layer_counts`: each entry counts the live leading slots of that index of sfc; they sum to 21, and at least one entry equals 4.
All inputs are finite; a program needn't handle non-finite values. No bound on the sum of `layer_counts` on one device may be relied on, other than what follows from the above.
Results may differ from a plain program's by a relative error of at most 0.00011.
Values sent between devices are 32-bit elements; how exact they have to be, the bound alone decides.
A program may use at most 64 MiB of HBM per device.

v0:
```python
import jax
import jax.numpy as jnp
from jax import lax
from jax.sharding import PartitionSpec as P

PRE_SWEEPS = 2
POST_SWEEPS = 2
COARSE_SWEEPS = 4


OMEGA = 2.0 / 3.0


def padded_2(cells, sides, width):
    for axis, dim in sides:
        count = lax.axis_size(axis)
        ends = count - 1
        head = lax.slice_in_dim(cells, 0, width, axis=dim)
        tail = lax.slice_in_dim(cells, cells.shape[dim] - width, cells.shape[dim], axis=dim)
        cells = jnp.concatenate(
            [
                lax.ppermute(tail, axis, [(i, (i + 1) % count) for i in range(ends)]),
                cells,
                lax.ppermute(head, axis, [((i + 1) % count, i) for i in range(ends)]),
            ],
            axis=dim,
        )
    return cells


def laplace(field, count, edge, outer_faces, side_faces):
    planes, width = field.shape
    plane = lax.broadcasted_iota(jnp.int32, (planes, 1), 0)
    last_index = count * edge - 1
    last = lax.dynamic_slice_in_dim(field, last_index, 1, 0)
    ends = outer_faces(jnp.concatenate([field[:1], last], axis=0))
    below = jnp.concatenate([ends[:1], field[:-1]], axis=0)
    above = jnp.concatenate([field[1:], jnp.zeros((1, width), jnp.float32)], axis=0)
    above = above + jnp.where(plane == last_index, ends[3:], 0.0)
    south, north = side_faces(
        jnp.concatenate([field[:, :edge], field[:, width - edge :]], axis=1), edge
    )
    north_rows = jnp.concatenate([field[:, edge:], north], axis=1)
    south_rows = jnp.concatenate([south, field[:, : width - edge]], axis=1)
    column = lax.broadcasted_iota(jnp.int32, (1, width), 1) % edge
    pad_col = jnp.zeros((planes, 1), jnp.float32)
    up_z = jnp.where(column != edge - 1, jnp.concatenate([field[:, 1:], pad_col], axis=1), 0.0)
    down_z = jnp.where(column != 0, jnp.concatenate([pad_col, field[:, :-1]], axis=1), 0.0)
    total = 6.0 * field - below - above - north_rows - south_rows - up_z - down_z
    return jnp.where(plane < count * edge, total, 0.0)


def padded_laplace(field, edge):
    planes, width = field.shape
    zero_plane = jnp.zeros((1, width), jnp.float32)
    below = jnp.concatenate([zero_plane, field[:-1]], axis=0)
    above = jnp.concatenate([field[1:], zero_plane], axis=0)
    pad_rows = jnp.zeros((planes, edge), jnp.float32)
    north_rows = jnp.concatenate([field[:, edge:], pad_rows], axis=1)
    south_rows = jnp.concatenate([pad_rows, field[:, : width - edge]], axis=1)
    column = lax.broadcasted_iota(jnp.int32, (1, width), 1) % edge
    pad_col = jnp.zeros((planes, 1), jnp.float32)
    up_z = jnp.where(column != edge - 1, jnp.concatenate([field[:, 1:], pad_col], axis=1), 0.0)
    down_z = jnp.where(column != 0, jnp.concatenate([pad_col, field[:, :-1]], axis=1), 0.0)
    return 6.0 * field - below - above - north_rows - south_rows - up_z - down_z


def deep_extend(stacked, count, edge, depth):
    kinds, planes, width = stacked.shape
    last = lax.dynamic_slice_in_dim(stacked, count * edge - depth, depth, 1)
    ends = jnp.concatenate([stacked[:, :depth], last], axis=1)
    got = padded_2(ends, (("sfc", 1),), depth)
    blank = jnp.zeros((kinds, depth, width), jnp.float32)
    extended = jnp.concatenate([got[:, :depth], stacked, blank], axis=1)
    extended = lax.dynamic_update_slice_in_dim(
        extended, got[:, 3 * depth :], depth + count * edge, 1
    )
    span = depth * edge
    faces = jnp.concatenate([extended[:, :, :span], extended[:, :, width - span :]], axis=2)
    wide = padded_2(faces, (("grp", 2),), span)
    return jnp.concatenate([wide[:, :, :span], extended, wide[:, :, 3 * span :]], axis=2)


def deep_mask(count, edge, depth, planes, width):
    span = depth * edge
    sfc_index = lax.axis_index("sfc")
    grp_index = lax.axis_index("grp")
    sfc_last = lax.axis_size("sfc") - 1
    grp_last = lax.axis_size("grp") - 1
    plane = lax.broadcasted_iota(jnp.int32, (planes + 2 * depth, 1), 0)
    live_end = depth + count * edge
    plane_ok = (plane < depth) & (sfc_index > 0) | (plane >= depth) & (plane < live_end)
    plane_ok = plane_ok | (plane >= live_end) & (plane < live_end + depth) & (sfc_index < sfc_last)
    column = lax.broadcasted_iota(jnp.int32, (1, width + 2 * span), 1)
    column_ok = (column < span) & (grp_index > 0) | (column >= span) & (column < span + width)
    column_ok = column_ok | (column >= span + width) & (grp_index < grp_last)
    return plane_ok & column_ok


def trim_live(padded, count, edge, depth, planes, width):
    span = depth * edge
    inner = padded[depth : depth + planes, span : span + width]
    plane = lax.broadcasted_iota(jnp.int32, (planes, 1), 0)
    return jnp.where(plane < count * edge, inner, 0.0)


def fine_ends(ends):
    return padded_2(ends, (("sfc", 0),), 1)


def fine_sides(faces, edge):
    wide = padded_2(faces, (("grp", 1),), edge)
    return (wide[:, :edge], wide[:, 3 * edge :])


def coarse_ends(ends):
    return padded_2(ends, (("sfc", 0),), 1)


def coarse_sides(faces, edge):
    wide = padded_2(faces, (("grp", 1),), edge)
    return (wide[:, :edge], wide[:, 3 * edge :])


def fine_laplace(field, count, edge):
    return laplace(field, count, edge, fine_ends, fine_sides)


def restrict(field, half):
    planes = field.shape[0]
    blocks = field.reshape(planes // 2, 2, half, 2, half, 2)
    return 0.125 * jnp.sum(blocks, axis=(1, 3, 5)).reshape(planes // 2, half * half)


def prolong(coarse, half):
    planes = coarse.shape[0]
    blocks = coarse.reshape(planes, 1, half, 1, half, 1)
    blocks = jnp.broadcast_to(blocks, (planes, 2, half, 2, half, 2))
    return blocks.reshape(planes * 2, 4 * half * half)


def coarse_solve(coarse_rhs, count, half):
    coarse_step = OMEGA / 1.5
    correction = coarse_step * coarse_rhs
    for sweep in range(COARSE_SWEEPS - 1):
        applied = laplace(correction, count, half, coarse_ends, coarse_sides)
        correction = correction + coarse_step * (coarse_rhs - 0.25 * applied)
    return correction


def vcycle(rhs, count, edge):
    step = OMEGA / 6.0
    half = edge // 2
    planes, width = rhs.shape
    depth = max(PRE_SWEEPS, POST_SWEEPS)
    keeper = deep_mask(count, edge, depth, planes, width)
    padded_rhs = deep_extend(rhs[None], count, edge, depth)[0]
    padded_z = step * padded_rhs
    padded_z = jnp.where(
        keeper, padded_z + step * (padded_rhs - padded_laplace(padded_z, edge)), 0.0
    )
    padded_defect = padded_rhs - padded_laplace(padded_z, edge)
    smooth = trim_live(padded_z, count, edge, depth, planes, width)
    defect = trim_live(padded_defect, count, edge, depth, planes, width)
    correction = coarse_solve(restrict(defect, half), count, half)
    smooth = smooth + prolong(correction, half)
    both = deep_extend(jnp.stack([rhs, smooth]), count, edge, depth)
    padded_rhs = both[0]
    padded_z = both[1]
    for sweep in range(POST_SWEEPS):
        padded_z = jnp.where(
            keeper, padded_z + step * (padded_rhs - padded_laplace(padded_z, edge)), 0.0
        )
    return trim_live(padded_z, count, edge, depth, planes, width)


def shards(source, layer_counts):
    count = layer_counts[0]
    slots, edge, width = source.shape
    planes = slots * edge
    plane = lax.broadcasted_iota(jnp.int32, (planes, 1), 0)
    first_rhs = jnp.where(plane < count * edge, source.reshape(planes, width), 0.0)
    first_z = vcycle(first_rhs, count, edge)
    rz_value = lax.psum(jnp.sum(first_rhs * first_z), ("sfc", "grp"))
    image = fine_laplace(first_z, count, edge)
    curv = lax.psum(jnp.sum(first_z * image), ("sfc", "grp"))
    alpha = rz_value / curv
    solution = alpha * first_z
    residual = first_rhs - alpha * image
    next_z = vcycle(residual, count, edge)
    cross = lax.psum(jnp.sum(next_z * image), ("sfc", "grp"))
    direction = next_z - cross / curv * first_z
    shape = (slots, edge, width)
    return (solution.reshape(shape), residual.reshape(shape), direction.reshape(shape))


def solution(mesh):
    return jax.shard_map(
        shards,
        mesh=mesh,
        in_specs=(P("sfc", None, "grp"), P("sfc")),
        out_specs=(P("sfc", None, "grp"), P("sfc", None, "grp"), P("sfc", None, "grp")),
        check_vma=False,
    )
```

profile of v0, /device:TPU:0, one launch (start us, length us, event | category | flops | bytes accessed | tf_op | source)
XLA Modules:
  0.0 298.7 jit_solution(9715950964302466820)
XLA Ops:
  4.5 5.5 %collective-permute-start = (f32[1,2,256]{2,1,0:T(2,128)S(1)}, f32[1,2,256]{2,1,0:T(2,128)S(1)}, u32[]{:S(2)}, u32[]{:S(2)}) collective-permute-start(f32[1,2,256]{2,1,0:T(2,128)S(1)} %fusion.88), channel_id=1, source_target_pairs={{0,4},{4,8},{8,12},{12,16},{16,20},{20,24},{24,28},{1,5},{5,9},{9,... | collective-permute-start | bytes 6152 | tf_op jit(solution)/shard_map/ppermute | solution.py:22
  14.2 3.9 %collective-permute-done.3 = f32[1,68,32]{2,1,0:T(8,128)S(1)} collective-permute-done((f32[1,68,32]{2,1,0:T(8,128)S(1)}, f32[1,68,32]{2,1,0:T(8,128)S(1)}, u32[]{:S(2)}, u32[]{:S(2)}) %collective-permute-start.3) | collective-permute-done | bytes 8736 | tf_op jit(solution)/shard_map/ppermute | solution.py:24
  19.1 5.6 %reshape.237 = f32[32,2,8,2,8,2]{5,4,3,2,1,0:T(8,128)} reshape(f32[64,256]{1,0:T(8,128)S(1)} %fusion.13) | data formatting | bytes 131072 | tf_op jit(solution)/shard_map/reshape | solution.py:131
  24.7 2.6 reduce_sum.45
  28.9 4.6 %collective-permute-start.7 = (f32[32,8]{0,1:T(8,128)S(1)}, f32[32,8]{0,1:T(8,128)S(1)}, u32[]{:S(2)}, u32[]{:S(2)}) collective-permute-start(f32[32,8]{0,1:T(8,128)S(1)} %get-tuple-element.142), channel_id=1, source_target_pairs={{0,1},{1,2},{2,3},{4,5},{5,6},{6,7},{8,9},{9,10},{10,11},{12,13},{... | collective-permute-start | bytes 3080 | tf_op jit(solution)/shard_map/ppermute | solution.py:22
  34.9 4.9 %collective-permute-start.4 = (f32[1,64]{0,1:T(8,128)S(1)}, f32[1,64]{0,1:T(8,128)S(1)}, u32[]{:S(2)}, u32[]{:S(2)}) collective-permute-start(f32[1,64]{0,1:T(8,128)S(1)} %constant_dynamic-slice_fusion.7), channel_id=1, source_target_pairs={{0,4},{4,8},{8,12},{12,16},{16,20},{20,24},{24,28},{1,5},{5,9},{9,... | collective-permute-start | bytes 776 | tf_op jit(solution)/shard_map/ppermute | solution.py:22
  46.6 5.7 %collective-permute-start.8 = (f32[1,64]{0,1:T(8,128)S(1)}, f32[1,64]{0,1:T(8,128)S(1)}, u32[]{:S(2)}, u32[]{:S(2)}) collective-permute-start(f32[1,64]{0,1:T(8,128)S(1)} %get-tuple-element.131), channel_id=1, source_target_pairs={{0,4},{4,8},{8,12},{12,16},{16,20},{20,24},{24,28},{1,5},{5,9},{9,... | collective-permute-start | bytes 776 | tf_op jit(solution)/shard_map/ppermute | solution.py:22
  54.2 3.7 %collective-permute-start.15 = (f32[32,8]{0,1:T(8,128)S(1)}, f32[32,8]{0,1:T(8,128)S(1)}, u32[]{:S(2)}, u32[]{:S(2)}) collective-permute-start(f32[32,8]{0,1:T(8,128)S(1)} %get-tuple-element.126), channel_id=1, source_target_pairs={{0,1},{1,2},{2,3},{4,5},{5,6},{6,7},{8,9},{9,10},{10,11},{12,13},{... | collective-permute-start | bytes 3080 | tf_op jit(solution)/shard_map/ppermute | solution.py:22
  60.5 5.8 %collective-permute-start.12 = (f32[1,64]{0,1:T(8,128)S(1)}, f32[1,64]{0,1:T(8,128)S(1)}, u32[]{:S(2)}, u32[]{:S(2)}) collective-permute-start(f32[1,64]{0,1:T(8,128)S(1)} %get-tuple-element.121), channel_id=1, source_target_pairs={{0,4},{4,8},{8,12},{12,16},{16,20},{20,24},{24,28},{1,5},{5,9},{9,... | collective-permute-start | bytes 776 | tf_op jit(solution)/shard_map/ppermute | solution.py:22
  70.4 4.0 %reshape.238 = f32[64,256]{1,0:T(8,128)S(1)} reshape(f32[32,2,8,2,8,2]{5,4,3,2,1,0:T(8,128)} %broadcast_in_dim.409) | data formatting | bytes 131072 | tf_op jit(solution)/shard_map/reshape | solution.py:139
  74.6 4.8 %collective-permute-start.16 = (f32[2,2,256]{2,1,0:T(2,128)S(1)}, f32[2,2,256]{2,1,0:T(2,128)S(1)}, u32[]{:S(2)}, u32[]{:S(2)}) collective-permute-start(f32[2,2,256]{2,1,0:T(2,128)S(1)} %get-tuple-element.31), channel_id=1, source_target_pairs={{0,4},{4,8},{8,12},{12,16},{16,20},{20,24},{24,28},{1,5},{5,9},{9,... | collective-permute-start | bytes 12296 | tf_op jit(solution)/shard_map/ppermute | solution.py:22
  80.9 5.4 %collective-permute-done.17 = f32[2,2,256]{2,1,0:T(2,128)S(1)} collective-permute-done((f32[2,2,256]{2,1,0:T(2,128)S(1)}, f32[2,2,256]{2,1,0:T(2,128)S(1)}, u32[]{:S(2)}, u32[]{:S(2)}) %collective-permute-start.17) | collective-permute-done | bytes 4128 | tf_op jit(solution)/shard_map/ppermute | solution.py:24
  86.3 3.1 %collective-permute-start.18 = (f32[2,68,32]{2,1,0:T(8,128)S(1)}, f32[2,68,32]{2,1,0:T(8,128)S(1)}, u32[]{:S(2)}, u32[]{:S(2)}) collective-permute-start(f32[2,68,32]{2,1,0:T(8,128)S(1)} %get-tuple-element.24), channel_id=1, source_target_pairs={{0,1},{1,2},{2,3},{4,5},{5,6},{6,7},{8,9},{9,10},{10,11},{12,13},{... | collective-permute-start | bytes 52232 | tf_op jit(solution)/shard_map/ppermute | solution.py:22
  90.7 5.4 %collective-permute-done.19 = f32[2,68,32]{2,1,0:T(8,128)S(1)} collective-permute-done((f32[2,68,32]{2,1,0:T(8,128)S(1)}, f32[2,68,32]{2,1,0:T(8,128)S(1)}, u32[]{:S(2)}, u32[]{:S(2)}) %collective-permute-start.19) | collective-permute-done | bytes 17440 | tf_op jit(solution)/shard_map/ppermute | solution.py:24
  97.4 4.8 %collective-permute-start.20 = (f32[1,256]{1,0:T(1,128)S(1)}, f32[1,256]{1,0:T(1,128)S(1)}, u32[]{:S(2)}, u32[]{:S(2)}) collective-permute-start(f32[1,256]{1,0:T(1,128)S(1)} %get-tuple-element.84), channel_id=1, source_target_pairs={{0,4},{4,8},{8,12},{12,16},{16,20},{20,24},{24,28},{1,5},{5,9},{9,... | collective-permute-start | bytes 3080 | tf_op jit(solution)/shard_map/ppermute | solution.py:22
  104.9 5.3 %collective-permute-start.23 = (f32[64,16]{1,0:T(8,128)S(1)}, f32[64,16]{1,0:T(8,128)S(1)}, u32[]{:S(2)}, u32[]{:S(2)}) collective-permute-start(f32[64,16]{1,0:T(8,128)S(1)} %get-tuple-element.91), channel_id=1, source_target_pairs={{0,1},{1,2},{2,3},{4,5},{5,6},{6,7},{8,9},{9,10},{10,11},{12,13},{... | collective-permute-start | bytes 12296 | tf_op jit(solution)/shard_map/ppermute | solution.py:22
  111.7 45.1 %all-reduce.69 = (f32[]{:T(128)}, f32[]{:T(128)}) all-reduce(f32[]{:T(128)} %get-tuple-element.4, f32[]{:T(128)} %get-tuple-element.3), channel_id=1, replica_groups=mesh['sfc'=8,'grp'=4] {'sfc','grp'}, use_global_device_ids=true, to_apply=%region_2.3 | all-reduce | flops 2 | bytes 16 | tf_op jit(solution)/shard_map/psum | solution.py:184
  158.3 4.2 %collective-permute-start.24 = (f32[1,2,256]{2,1,0:T(2,128)S(1)}, f32[1,2,256]{2,1,0:T(2,128)S(1)}, u32[]{:S(2)}, u32[]{:S(2)}) collective-permute-start(f32[1,2,256]{2,1,0:T(2,128)S(1)} %fusion.89), channel_id=1, source_target_pairs={{0,4},{4,8},{8,12},{12,16},{16,20},{20,24},{24,28},{1,5},{5,9},{9,... | collective-permute-start | bytes 6152 | tf_op jit(solution)/shard_map/ppermute | solution.py:22
  163.9 4.1 %collective-permute-done.25 = f32[1,2,256]{2,1,0:T(2,128)S(1)} collective-permute-done((f32[1,2,256]{2,1,0:T(2,128)S(1)}, f32[1,2,256]{2,1,0:T(2,128)S(1)}, u32[]{:S(2)}, u32[]{:S(2)}) %collective-permute-start.25) | collective-permute-done | bytes 2080 | tf_op jit(solution)/shard_map/ppermute | solution.py:24
  174.1 5.6 %reshape.241 = f32[32,2,8,2,8,2]{5,4,3,2,1,0:T(8,128)} reshape(f32[64,256]{1,0:T(8,128)S(1)} %fusion.4) | data formatting | bytes 131072 | tf_op jit(solution)/shard_map/reshape | solution.py:131
  179.7 2.6 reduce_sum.48
  182.5 4.6 %collective-permute-start.31 = (f32[32,8]{0,1:T(8,128)S(1)}, f32[32,8]{0,1:T(8,128)S(1)}, u32[]{:S(2)}, u32[]{:S(2)}) collective-permute-start(f32[32,8]{0,1:T(8,128)S(1)} %get-tuple-element.116), channel_id=1, source_target_pairs={{0,1},{1,2},{2,3},{4,5},{5,6},{6,7},{8,9},{9,10},{10,11},{12,13},{... | collective-permute-start | bytes 3080 | tf_op jit(solution)/shard_map/ppermute | solution.py:22
  190.0 4.5 %collective-permute-start.28 = (f32[1,64]{0,1:T(8,128)S(1)}, f32[1,64]{0,1:T(8,128)S(1)}, u32[]{:S(2)}, u32[]{:S(2)}) collective-permute-start(f32[1,64]{0,1:T(8,128)S(1)} %constant_dynamic-slice_fusion.2), channel_id=1, source_target_pairs={{0,4},{4,8},{8,12},{12,16},{16,20},{20,24},{24,28},{1,5},{5,9},{9,... | collective-permute-start | bytes 776 | tf_op jit(solution)/shard_map/ppermute | solution.py:22
  201.3 5.1 %collective-permute-start.32 = (f32[1,64]{0,1:T(8,128)S(1)}, f32[1,64]{0,1:T(8,128)S(1)}, u32[]{:S(2)}, u32[]{:S(2)}) collective-permute-start(f32[1,64]{0,1:T(8,128)S(1)} %get-tuple-element.105), channel_id=1, source_target_pairs={{0,4},{4,8},{8,12},{12,16},{16,20},{20,24},{24,28},{1,5},{5,9},{9,... | collective-permute-start | bytes 776 | tf_op jit(solution)/shard_map/ppermute | solution.py:22
  208.3 4.0 %collective-permute-start.39 = (f32[32,8]{0,1:T(8,128)S(1)}, f32[32,8]{0,1:T(8,128)S(1)}, u32[]{:S(2)}, u32[]{:S(2)}) collective-permute-start(f32[32,8]{0,1:T(8,128)S(1)} %get-tuple-element.100), channel_id=1, source_target_pairs={{0,1},{1,2},{2,3},{4,5},{5,6},{6,7},{8,9},{9,10},{10,11},{12,13},{... | collective-permute-start | bytes 3080 | tf_op jit(solution)/shard_map/ppermute | solution.py:22
  215.1 5.8 %collective-permute-start.36 = (f32[1,64]{0,1:T(8,128)S(1)}, f32[1,64]{0,1:T(8,128)S(1)}, u32[]{:S(2)}, u32[]{:S(2)}) collective-permute-start(f32[1,64]{0,1:T(8,128)S(1)} %get-tuple-element.95), channel_id=1, source_target_pairs={{0,4},{4,8},{8,12},{12,16},{16,20},{20,24},{24,28},{1,5},{5,9},{9,... | collective-permute-start | bytes 776 | tf_op jit(solution)/shard_map/ppermute | solution.py:22
  225.0 4.0 %reshape.242 = f32[64,256]{1,0:T(8,128)S(1)} reshape(f32[32,2,8,2,8,2]{5,4,3,2,1,0:T(8,128)} %broadcast_in_dim.422) | data formatting | bytes 131072 | tf_op jit(solution)/shard_map/reshape | solution.py:139
  229.2 4.8 %collective-permute-start.40 = (f32[2,2,256]{2,1,0:T(2,128)S(1)}, f32[2,2,256]{2,1,0:T(2,128)S(1)}, u32[]{:S(2)}, u32[]{:S(2)}) collective-permute-start(f32[2,2,256]{2,1,0:T(2,128)S(1)} %get-tuple-element.27), channel_id=1, source_target_pairs={{0,4},{4,8},{8,12},{12,16},{16,20},{20,24},{24,28},{1,5},{5,9},{9,... | collective-permute-start | bytes 12296 | tf_op jit(solution)/shard_map/ppermute | solution.py:22
  235.4 5.4 %collective-permute-done.41 = f32[2,2,256]{2,1,0:T(2,128)S(1)} collective-permute-done((f32[2,2,256]{2,1,0:T(2,128)S(1)}, f32[2,2,256]{2,1,0:T(2,128)S(1)}, u32[]{:S(2)}, u32[]{:S(2)}) %collective-permute-start.41) | collective-permute-done | bytes 4128 | tf_op jit(solution)/shard_map/ppermute | solution.py:24
  240.9 3.1 %collective-permute-start.42 = (f32[2,68,32]{2,1,0:T(8,128)S(1)}, f32[2,68,32]{2,1,0:T(8,128)S(1)}, u32[]{:S(2)}, u32[]{:S(2)}) collective-permute-start(f32[2,68,32]{2,1,0:T(8,128)S(1)} %get-tuple-element.22), channel_id=1, source_target_pairs={{0,1},{1,2},{2,3},{4,5},{5,6},{6,7},{8,9},{9,10},{10,11},{12,13},{... | collective-permute-start | bytes 52232 | tf_op jit(solution)/shard_map/ppermute | solution.py:22
  245.3 5.4 %collective-permute-done.43 = f32[2,68,32]{2,1,0:T(8,128)S(1)} collective-permute-done((f32[2,68,32]{2,1,0:T(8,128)S(1)}, f32[2,68,32]{2,1,0:T(8,128)S(1)}, u32[]{:S(2)}, u32[]{:S(2)}) %collective-permute-start.43) | collective-permute-done | bytes 17440 | tf_op jit(solution)/shard_map/ppermute | solution.py:24
  252.4 44.3 %psum.23 = f32[]{:T(128)} all-reduce(f32[]{:T(128)} %get-tuple-element.7), channel_id=1, replica_groups=mesh['sfc'=8,'grp'=4] {'sfc','grp'}, use_global_device_ids=true, to_apply=%region_7.8 | all-reduce | flops 1 | bytes 8 | tf_op jit(solution)/shard_map/psum | solution.py:191
  (213 shorter events, 65.9 us)
Async XLA Ops:
  2.2 9.1 %collective-permute-start.1 = (f32[1,2,256]{2,1,0:T(2,128)S(1)}, f32[1,2,256]{2,1,0:T(2,128)S(1)}, u32[]{:S(2)}, u32[]{:S(2)}) collective-permute-start(f32[1,2,256]{2,1,0:T(2,128)S(1)} %slice.576), channel_id=1, source_target_pairs={{4,0},{8,4},{12,8},{16,12},{20,16},{24,20},{28,24},{5,1},{9,5},{13... | collective-permute-start | bytes 6152 | tf_op jit(solution)/shard_map/ppermute | solution.py:24
  4.5 6.8 %collective-permute-start = (f32[1,2,256]{2,1,0:T(2,128)S(1)}, f32[1,2,256]{2,1,0:T(2,128)S(1)}, u32[]{:S(2)}, u32[]{:S(2)}) collective-permute-start(f32[1,2,256]{2,1,0:T(2,128)S(1)} %fusion.88), channel_id=1, source_target_pairs={{0,4},{4,8},{8,12},{12,16},{16,20},{20,24},{24,28},{1,5},{5,9},{9,... | collective-permute-start | bytes 6152 | tf_op jit(solution)/shard_map/ppermute | solution.py:22
  27.6 12.4 %collective-permute-start.5 = (f32[1,64]{1,0:T(1,128)S(1)}, f32[1,64]{1,0:T(1,128)S(1)}, u32[]{:S(2)}, u32[]{:S(2)}) collective-permute-start(f32[1,64]{1,0:T(1,128)S(1)} %slice.455), channel_id=1, source_target_pairs={{4,0},{8,4},{12,8},{16,12},{20,16},{24,20},{28,24},{5,1},{9,5},{13... | collective-permute-start | bytes 776 | tf_op jit(solution)/shard_map/ppermute | solution.py:24
  28.9 12.5 %collective-permute-start.7 = (f32[32,8]{0,1:T(8,128)S(1)}, f32[32,8]{0,1:T(8,128)S(1)}, u32[]{:S(2)}, u32[]{:S(2)}) collective-permute-start(f32[32,8]{0,1:T(8,128)S(1)} %get-tuple-element.142), channel_id=1, source_target_pairs={{0,1},{1,2},{2,3},{4,5},{5,6},{6,7},{8,9},{9,10},{10,11},{12,13},{... | collective-permute-start | bytes 3080 | tf_op jit(solution)/shard_map/ppermute | solution.py:22
  33.5 7.9 %collective-permute-start.6 = (f32[32,8]{0,1:T(8,128)S(1)}, f32[32,8]{0,1:T(8,128)S(1)}, u32[]{:S(2)}, u32[]{:S(2)}) collective-permute-start(f32[32,8]{0,1:T(8,128)S(1)} %get-tuple-element.143), channel_id=1, source_target_pairs={{1,0},{2,1},{3,2},{5,4},{6,5},{7,6},{9,8},{10,9},{11,10},{13,12},{... | collective-permute-start | bytes 3080 | tf_op jit(solution)/shard_map/ppermute | solution.py:24
  34.9 6.5 %collective-permute-start.4 = (f32[1,64]{0,1:T(8,128)S(1)}, f32[1,64]{0,1:T(8,128)S(1)}, u32[]{:S(2)}, u32[]{:S(2)}) collective-permute-start(f32[1,64]{0,1:T(8,128)S(1)} %constant_dynamic-slice_fusion.7), channel_id=1, source_target_pairs={{0,4},{4,8},{8,12},{12,16},{16,20},{20,24},{24,28},{1,5},{5,9},{9,... | collective-permute-start | bytes 776 | tf_op jit(solution)/shard_map/ppermute | solution.py:22
  41.7 12.2 %collective-permute-start.11 = (f32[32,8]{0,1:T(8,128)S(1)}, f32[32,8]{0,1:T(8,128)S(1)}, u32[]{:S(2)}, u32[]{:S(2)}) collective-permute-start(f32[32,8]{0,1:T(8,128)S(1)} %get-tuple-element.136), channel_id=1, source_target_pairs={{0,1},{1,2},{2,3},{4,5},{5,6},{6,7},{8,9},{9,10},{10,11},{12,13},{... | collective-permute-start | bytes 3080 | tf_op jit(solution)/shard_map/ppermute | solution.py:22
  44.0 9.9 %collective-permute-start.10 = (f32[32,8]{0,1:T(8,128)S(1)}, f32[32,8]{0,1:T(8,128)S(1)}, u32[]{:S(2)}, u32[]{:S(2)}) collective-permute-start(f32[32,8]{0,1:T(8,128)S(1)} %get-tuple-element.137), channel_id=1, source_target_pairs={{1,0},{2,1},{3,2},{5,4},{6,5},{7,6},{9,8},{10,9},{11,10},{13,12},{... | collective-permute-start | bytes 3080 | tf_op jit(solution)/shard_map/ppermute | solution.py:24
  45.3 7.0 %collective-permute-start.9 = (f32[1,64]{0,1:T(8,128)S(1)}, f32[1,64]{0,1:T(8,128)S(1)}, u32[]{:S(2)}, u32[]{:S(2)}) collective-permute-start(f32[1,64]{0,1:T(8,128)S(1)} %get-tuple-element.130), channel_id=1, source_target_pairs={{4,0},{8,4},{12,8},{16,12},{20,16},{24,20},{28,24},{5,1},{9,5},{13... | collective-permute-start | bytes 776 | tf_op jit(solution)/shard_map/ppermute | solution.py:24
  46.6 7.3 %collective-permute-start.8 = (f32[1,64]{0,1:T(8,128)S(1)}, f32[1,64]{0,1:T(8,128)S(1)}, u32[]{:S(2)}, u32[]{:S(2)}) collective-permute-start(f32[1,64]{0,1:T(8,128)S(1)} %get-tuple-element.131), channel_id=1, source_target_pairs={{0,4},{4,8},{8,12},{12,16},{16,20},{20,24},{24,28},{1,5},{5,9},{9,... | collective-permute-start | bytes 776 | tf_op jit(solution)/shard_map/ppermute | solution.py:22
  54.2 13.6 %collective-permute-start.15 = (f32[32,8]{0,1:T(8,128)S(1)}, f32[32,8]{0,1:T(8,128)S(1)}, u32[]{:S(2)}, u32[]{:S(2)}) collective-permute-start(f32[32,8]{0,1:T(8,128)S(1)} %get-tuple-element.126), channel_id=1, source_target_pairs={{0,1},{1,2},{2,3},{4,5},{5,6},{6,7},{8,9},{9,10},{10,11},{12,13},{... | collective-permute-start | bytes 3080 | tf_op jit(solution)/shard_map/ppermute | solution.py:22
  57.9 9.9 %collective-permute-start.14 = (f32[32,8]{0,1:T(8,128)S(1)}, f32[32,8]{0,1:T(8,128)S(1)}, u32[]{:S(2)}, u32[]{:S(2)}) collective-permute-start(f32[32,8]{0,1:T(8,128)S(1)} %get-tuple-element.127), channel_id=1, source_target_pairs={{1,0},{2,1},{3,2},{5,4},{6,5},{7,6},{9,8},{10,9},{11,10},{13,12},{... | collective-permute-start | bytes 3080 | tf_op jit(solution)/shard_map/ppermute | solution.py:24
  59.2 7.1 %collective-permute-start.13 = (f32[1,64]{0,1:T(8,128)S(1)}, f32[1,64]{0,1:T(8,128)S(1)}, u32[]{:S(2)}, u32[]{:S(2)}) collective-permute-start(f32[1,64]{0,1:T(8,128)S(1)} %get-tuple-element.120), channel_id=1, source_target_pairs={{4,0},{8,4},{12,8},{16,12},{20,16},{24,20},{28,24},{5,1},{9,5},{13... | collective-permute-start | bytes 776 | tf_op jit(solution)/shard_map/ppermute | solution.py:24
  60.5 7.3 %collective-permute-start.12 = (f32[1,64]{0,1:T(8,128)S(1)}, f32[1,64]{0,1:T(8,128)S(1)}, u32[]{:S(2)}, u32[]{:S(2)}) collective-permute-start(f32[1,64]{0,1:T(8,128)S(1)} %get-tuple-element.121), channel_id=1, source_target_pairs={{0,4},{4,8},{8,12},{12,16},{16,20},{20,24},{24,28},{1,5},{5,9},{9,... | collective-permute-start | bytes 776 | tf_op jit(solution)/shard_map/ppermute | solution.py:22
  79.5 6.8 %collective-permute-start.17 = (f32[2,2,256]{2,1,0:T(2,128)S(1)}, f32[2,2,256]{2,1,0:T(2,128)S(1)}, u32[]{:S(2)}, u32[]{:S(2)}) collective-permute-start(f32[2,2,256]{2,1,0:T(2,128)S(1)} %get-tuple-element.30), channel_id=1, source_target_pairs={{4,0},{8,4},{12,8},{16,12},{20,16},{24,20},{28,24},{5,1},{9,5},{13... | collective-permute-start | bytes 12296 | tf_op jit(solution)/shard_map/ppermute | solution.py:24
  89.4 6.7 %collective-permute-start.19 = (f32[2,68,32]{2,1,0:T(8,128)S(1)}, f32[2,68,32]{2,1,0:T(8,128)S(1)}, u32[]{:S(2)}, u32[]{:S(2)}) collective-permute-start(f32[2,68,32]{2,1,0:T(8,128)S(1)} %get-tuple-element.25), channel_id=1, source_target_pairs={{1,0},{2,1},{3,2},{5,4},{6,5},{7,6},{9,8},{10,9},{11,10},{13,12},{... | collective-permute-start | bytes 52232 | tf_op jit(solution)/shard_map/ppermute | solution.py:24
  97.4 12.7 %collective-permute-start.20 = (f32[1,256]{1,0:T(1,128)S(1)}, f32[1,256]{1,0:T(1,128)S(1)}, u32[]{:S(2)}, u32[]{:S(2)}) collective-permute-start(f32[1,256]{1,0:T(1,128)S(1)} %get-tuple-element.84), channel_id=1, source_target_pairs={{0,4},{4,8},{8,12},{12,16},{16,20},{20,24},{24,28},{1,5},{5,9},{9,... | collective-permute-start | bytes 3080 | tf_op jit(solution)/shard_map/ppermute | solution.py:22
  102.3 7.9 %collective-permute-start.21 = (f32[1,256]{1,0:T(1,128)S(1)}, f32[1,256]{1,0:T(1,128)S(1)}, u32[]{:S(2)}, u32[]{:S(2)}) collective-permute-start(f32[1,256]{1,0:T(1,128)S(1)} %get-tuple-element.85), channel_id=1, source_target_pairs={{4,0},{8,4},{12,8},{16,12},{20,16},{24,20},{28,24},{5,1},{9,5},{13... | collective-permute-start | bytes 3080 | tf_op jit(solution)/shard_map/ppermute | solution.py:24
  103.6 6.6 %collective-permute-start.22 = (f32[64,16]{1,0:T(8,128)S(1)}, f32[64,16]{1,0:T(8,128)S(1)}, u32[]{:S(2)}, u32[]{:S(2)}) collective-permute-start(f32[64,16]{1,0:T(8,128)S(1)} %get-tuple-element.90), channel_id=1, source_target_pairs={{1,0},{2,1},{3,2},{5,4},{6,5},{7,6},{9,8},{10,9},{11,10},{13,12},{... | collective-permute-start | bytes 12296 | tf_op jit(solution)/shard_map/ppermute | solution.py:24
  182.5 13.6 %collective-permute-start.31 = (f32[32,8]{0,1:T(8,128)S(1)}, f32[32,8]{0,1:T(8,128)S(1)}, u32[]{:S(2)}, u32[]{:S(2)}) collective-permute-start(f32[32,8]{0,1:T(8,128)S(1)} %get-tuple-element.116), channel_id=1, source_target_pairs={{0,1},{1,2},{2,3},{4,5},{5,6},{6,7},{8,9},{9,10},{10,11},{12,13},{... | collective-permute-start | bytes 3080 | tf_op jit(solution)/shard_map/ppermute | solution.py:22
  187.1 9.1 %collective-permute-start.30 = (f32[32,8]{0,1:T(8,128)S(1)}, f32[32,8]{0,1:T(8,128)S(1)}, u32[]{:S(2)}, u32[]{:S(2)}) collective-permute-start(f32[32,8]{0,1:T(8,128)S(1)} %get-tuple-element.117), channel_id=1, source_target_pairs={{1,0},{2,1},{3,2},{5,4},{6,5},{7,6},{9,8},{10,9},{11,10},{13,12},{... | collective-permute-start | bytes 3080 | tf_op jit(solution)/shard_map/ppermute | solution.py:24
  190.0 6.2 %collective-permute-start.28 = (f32[1,64]{0,1:T(8,128)S(1)}, f32[1,64]{0,1:T(8,128)S(1)}, u32[]{:S(2)}, u32[]{:S(2)}) collective-permute-start(f32[1,64]{0,1:T(8,128)S(1)} %constant_dynamic-slice_fusion.2), channel_id=1, source_target_pairs={{0,4},{4,8},{8,12},{12,16},{16,20},{20,24},{24,28},{1,5},{5,9},{9,... | collective-permute-start | bytes 776 | tf_op jit(solution)/shard_map/ppermute | solution.py:22
  196.5 11.5 %collective-permute-start.35 = (f32[32,8]{0,1:T(8,128)S(1)}, f32[32,8]{0,1:T(8,128)S(1)}, u32[]{:S(2)}, u32[]{:S(2)}) collective-permute-start(f32[32,8]{0,1:T(8,128)S(1)} %get-tuple-element.110), channel_id=1, source_target_pairs={{0,1},{1,2},{2,3},{4,5},{5,6},{6,7},{8,9},{9,10},{10,11},{12,13},{... | collective-permute-start | bytes 3080 | tf_op jit(solution)/shard_map/ppermute | solution.py:22
  198.7 9.3 %collective-permute-start.34 = (f32[32,8]{0,1:T(8,128)S(1)}, f32[32,8]{0,1:T(8,128)S(1)}, u32[]{:S(2)}, u32[]{:S(2)}) collective-permute-start(f32[32,8]{0,1:T(8,128)S(1)} %get-tuple-element.111), channel_id=1, source_target_pairs={{1,0},{2,1},{3,2},{5,4},{6,5},{7,6},{9,8},{10,9},{11,10},{13,12},{... | collective-permute-start | bytes 3080 | tf_op jit(solution)/shard_map/ppermute | solution.py:24
  200.0 6.4 %collective-permute-start.33 = (f32[1,64]{0,1:T(8,128)S(1)}, f32[1,64]{0,1:T(8,128)S(1)}, u32[]{:S(2)}, u32[]{:S(2)}) collective-permute-start(f32[1,64]{0,1:T(8,128)S(1)} %get-tuple-element.104), channel_id=1, source_target_pairs={{4,0},{8,4},{12,8},{16,12},{20,16},{24,20},{28,24},{5,1},{9,5},{13... | collective-permute-start | bytes 776 | tf_op jit(solution)/shard_map/ppermute | solution.py:24
  201.3 6.7 %collective-permute-start.32 = (f32[1,64]{0,1:T(8,128)S(1)}, f32[1,64]{0,1:T(8,128)S(1)}, u32[]{:S(2)}, u32[]{:S(2)}) collective-permute-start(f32[1,64]{0,1:T(8,128)S(1)} %get-tuple-element.105), channel_id=1, source_target_pairs={{0,4},{4,8},{8,12},{12,16},{16,20},{20,24},{24,28},{1,5},{5,9},{9,... | collective-permute-start | bytes 776 | tf_op jit(solution)/shard_map/ppermute | solution.py:22
  208.3 14.1 %collective-permute-start.39 = (f32[32,8]{0,1:T(8,128)S(1)}, f32[32,8]{0,1:T(8,128)S(1)}, u32[]{:S(2)}, u32[]{:S(2)}) collective-permute-start(f32[32,8]{0,1:T(8,128)S(1)} %get-tuple-element.100), channel_id=1, source_target_pairs={{0,1},{1,2},{2,3},{4,5},{5,6},{6,7},{8,9},{9,10},{10,11},{12,13},{... | collective-permute-start | bytes 3080 | tf_op jit(solution)/shard_map/ppermute | solution.py:22
  212.3 10.1 %collective-permute-start.38 = (f32[32,8]{0,1:T(8,128)S(1)}, f32[32,8]{0,1:T(8,128)S(1)}, u32[]{:S(2)}, u32[]{:S(2)}) collective-permute-start(f32[32,8]{0,1:T(8,128)S(1)} %get-tuple-element.101), channel_id=1, source_target_pairs={{1,0},{2,1},{3,2},{5,4},{6,5},{7,6},{9,8},{10,9},{11,10},{13,12},{... | collective-permute-start | bytes 3080 | tf_op jit(solution)/shard_map/ppermute | solution.py:24
  213.6 7.3 %collective-permute-start.37 = (f32[1,64]{0,1:T(8,128)S(1)}, f32[1,64]{0,1:T(8,128)S(1)}, u32[]{:S(2)}, u32[]{:S(2)}) collective-permute-start(f32[1,64]{0,1:T(8,128)S(1)} %get-tuple-element.94), channel_id=1, source_target_pairs={{4,0},{8,4},{12,8},{16,12},{20,16},{24,20},{28,24},{5,1},{9,5},{13... | collective-permute-start | bytes 776 | tf_op jit(solution)/shard_map/ppermute | solution.py:24
  215.1 7.3 %collective-permute-start.36 = (f32[1,64]{0,1:T(8,128)S(1)}, f32[1,64]{0,1:T(8,128)S(1)}, u32[]{:S(2)}, u32[]{:S(2)}) collective-permute-start(f32[1,64]{0,1:T(8,128)S(1)} %get-tuple-element.95), channel_id=1, source_target_pairs={{0,4},{4,8},{8,12},{12,16},{16,20},{20,24},{24,28},{1,5},{5,9},{9,... | collective-permute-start | bytes 776 | tf_op jit(solution)/shard_map/ppermute | solution.py:22
  234.0 6.8 %collective-permute-start.41 = (f32[2,2,256]{2,1,0:T(2,128)S(1)}, f32[2,2,256]{2,1,0:T(2,128)S(1)}, u32[]{:S(2)}, u32[]{:S(2)}) collective-permute-start(f32[2,2,256]{2,1,0:T(2,128)S(1)} %get-tuple-element.26), channel_id=1, source_target_pairs={{4,0},{8,4},{12,8},{16,12},{20,16},{24,20},{28,24},{5,1},{9,5},{13... | collective-permute-start | bytes 12296 | tf_op jit(solution)/shard_map/ppermute | solution.py:24
  244.0 6.7 %collective-permute-start.43 = (f32[2,68,32]{2,1,0:T(8,128)S(1)}, f32[2,68,32]{2,1,0:T(8,128)S(1)}, u32[]{:S(2)}, u32[]{:S(2)}) collective-permute-start(f32[2,68,32]{2,1,0:T(8,128)S(1)} %get-tuple-element.23), channel_id=1, source_target_pairs={{1,0},{2,1},{3,2},{5,4},{6,5},{7,6},{9,8},{10,9},{11,10},{13,12},{... | collective-permute-start | bytes 52232 | tf_op jit(solution)/shard_map/ppermute | solution.py:24
  (14 other events, 172.4 us)
where the time goes:
time: 300 us; the launch traced here: 299 us
  starting transfers between devices  120 us (40%)
  blocking collectives  89.4 us (30%)
  waiting for transfers between devices  42.4 us (14%)
  local copies, waits for them, and re-layouts  28.7 us (10%)
  other arithmetic  13.1 us (4%)
  between operations  5.23 us (2%)
    ppermute x22, starting transfers between devices, padded_2(): lax.ppermute(tail, axis, [(i, (i + 1) % count) for i in range(ends)])  91.2 us
    psum x1, blocking collectives, shards(): rz_value = lax.psum(jnp.sum(first_rhs * first_z), ('sfc', 'grp'))  45.1 us
    psum x1, blocking collectives, shards(): cross = lax.psum(jnp.sum(next_z * image), ('sfc', 'grp'))  44.3 us
    ppermute x22, waiting for transfers between devices, padded_2(): lax.ppermute(head, axis, [((i + 1) % count, i) for i in range(ends)])  32.1 us
    ppermute x22, starting transfers between devices, padded_2(): lax.ppermute(head, axis, [((i + 1) % count, i) for i in range(ends)])  28.6 us
    reshape x2, local copies, waits for them, and re-layouts, restrict(): blocks = field.reshape(planes // 2, 2, half, 2, half, 2)  11.2 us
    ppermute x22, waiting for transfers between devices, padded_2(): lax.ppermute(tail, axis, [(i, (i + 1) % count) for i in range(ends)])  10.4 us
    reshape x2, local copies, waits for them, and re-layouts, prolong(): return blocks.reshape(planes * 2, 4 * half * half)  8.07 us
  transfers between devices with their start and end apart: 44, of which 15 were waited for; matrix products, arithmetic and copies ran while one was open for 1% of the time, Pallas kernels for 0%

commit v1 on v0

v1 whole, which is shorter than its diff:
```python
import functools

import jax
import jax.numpy as jnp
from jax import lax
from jax.experimental import pallas as pl
from jax.experimental.pallas import tpu as pltpu
from jax.sharding import PartitionSpec as P

MESH = pl.DeviceIdType.MESH
OMEGA = 2.0 / 3.0
LANES = 128
SUBS = 8
COARSE_SWEEPS = 4
POST_SWEEPS = 2
WAYS = ((0, 1), (0, -1), (1, 0), (1, 1), (1, -1), (-1, 0), (-1, 1), (-1, -1))


def kernel(
    dims, count_ref, source_ref, solution_ref, residual_ref, direction_ref,
    rhs, smooth, other, coarse, ea, eb, mask, image_ref, first_ref, last,
    side, below, above, part, total, red_grp, red_sfc,
    send_sem, recv_sem, grp_send, grp_recv, sfc_send, sfc_recv,
):
    slots, edge, tiles, n_sfc, n_grp = dims
    planes = slots * edge
    sfc = lax.axis_index("sfc")
    grp = lax.axis_index("grp")
    count = count_ref[0]
    step = OMEGA / 6.0
    cstep = OMEGA / 1.5
    middle = (SUBS - tiles) // 2

    def there(ds, dg):
        flag = None
        if ds:
            flag = sfc < n_sfc - 1 if ds > 0 else sfc > 0
        if dg:
            extra = grp < n_grp - 1 if dg > 0 else grp > 0
            flag = extra if flag is None else jnp.logical_and(flag, extra)
        return flag

    barrier = pltpu.get_barrier_semaphore()

    def greet(i, axis, size, me):
        pl.semaphore_signal(
            barrier, inc=1, device_id={axis: lax.rem(me + i, size)}, device_id_type=MESH
        )

    for i in range(1, n_grp):
        greet(i, "grp", n_grp, grp)

    def greet_sfc(i, carry):
        greet(i, "sfc", n_sfc, sfc)
        return carry

    lax.fori_loop(1, n_sfc, greet_sfc, 0)
    for ds, dg in WAYS:
        if ds and dg:
            @pl.when(there(ds, dg))
            def _():
                pl.semaphore_signal(
                    barrier, inc=1, device_id={"sfc": sfc + ds, "grp": grp + dg},
                    device_id_type=MESH,
                )

    def one(flag):
        return jnp.where(flag, 1, 0)

    diagonals = (one(sfc > 0) + one(sfc < n_sfc - 1)) * (one(grp > 0) + one(grp < n_grp - 1))

    lane = lax.broadcasted_iota(jnp.int32, (1, SUBS, LANES), 2)
    sub = lax.broadcasted_iota(jnp.int32, (1, SUBS, LANES), 1)
    z = lane % edge

    def has(flag_int):
        return flag_int > 0

    has_below = one(sfc > 0)
    has_above = one(sfc < n_sfc - 1)
    has_left = one(grp > 0)
    has_right = one(grp < n_grp - 1)
    owned = jnp.logical_and(sub >= middle, sub < middle + tiles)
    lefts = jnp.logical_and(sub >= middle - tiles, sub < middle)
    rights = jnp.logical_and(sub >= middle + tiles, sub < middle + 2 * tiles)
    rows_ok = (
        jnp.where(owned, 1, 0) + jnp.where(lefts, 1, 0) * has_left
        + jnp.where(rights, 1, 0) * has_right
    )
    for s in range(slots + 2):
        if s == 0:
            ok = has_below
        else:
            ok = one(count >= s) + one(count == s - 1) * has_above
        mask[pl.ds(SUBS * s, SUBS), :] = (rows_ok * ok).astype(jnp.float32)[0]

    def zero_rhs(i, carry):
        rhs[pl.ds(i * SUBS, SUBS), :] = jnp.zeros((SUBS, LANES), jnp.float32)
        return carry

    lax.fori_loop(0, planes + 2 * edge + 2, zero_rhs, 0)

    def fill_last(src):
        value = src[pl.ds(0, edge), :]
        for s in range(1, slots):
            value = jnp.where(count > s, src[pl.ds(s * edge, edge), :], value)
        last[...] = value

    def copies(e, i, ds, dg, src):
        gpos = 1 - dg
        if ds == 0:
            source, target = src, side.at[e, gpos // 2]
        elif ds > 0:
            source, target = last.at[e], below.at[e, gpos]
        else:
            source, target = src.at[pl.ds(0, edge)], above.at[e, gpos]
        return pltpu.make_async_remote_copy(
            src_ref=source, dst_ref=target, send_sem=send_sem.at[e, i],
            recv_sem=recv_sem.at[e, i], device_id={"sfc": sfc + ds, "grp": grp + dg},
            device_id_type=MESH,
        )

    def start(e, src):
        for i, (ds, dg) in enumerate(WAYS):
            @pl.when(there(ds, dg))
            def _(i=i, ds=ds, dg=dg):
                copies(e, i, ds, dg, src).start()

    def receive(e, src):
        for i, (ds, dg) in enumerate(WAYS):
            @pl.when(there(-ds, -dg))
            def _(i=i, ds=ds, dg=dg):
                copies(e, i, ds, dg, src).wait_recv()

    def sent(e, src):
        for i, (ds, dg) in enumerate(WAYS):
            @pl.when(there(ds, dg))
            def _(i=i, ds=ds, dg=dg):
                copies(e, i, ds, dg, src).wait_send()

    def pick_last(e, src):
        value = src[pl.ds(0, edge), :]
        for s in range(1, slots):
            value = jnp.where(count > s, src[pl.ds(s * edge, edge), :], value)
        last[e] = value

    def unpack(e, src):
        sides = ((0, has_left), (1, 1), (2, has_right))
        for g, present in sides:
            for s in range(slots + 2):
                for h in range(edge // SUBS):
                    for t in range(tiles):
                        cols = pl.ds(t * LANES, LANES)
                        rows = pl.ds(h * SUBS, SUBS)

                        def centre(slot):
                            at = pl.ds(slot * edge + h * SUBS, SUBS)
                            return src[at, cols] if g == 1 else side[e, g // 2, at, cols]

                        if s == 0:
                            value = jnp.where(has(has_below * present), below[e, g, rows, cols], 0.0)
                        else:
                            up = one(count == s - 1) * has_above * present
                            value = jnp.zeros((SUBS, LANES), jnp.float32)
                            if s >= 2:
                                value = jnp.where(has(up), above[e, g, rows, cols], value)
                            if s <= slots:
                                value = jnp.where(has(one(count >= s) * present), centre(s - 1), value)
                        plane = 1 + s * edge + h * SUBS
                        at_sub = middle + (g - 1) * tiles + t
                        rhs[pl.ds(plane * SUBS + at_sub, SUBS, stride=SUBS), :] = value

    def roll(v, amount, axis):
        return pltpu.roll(v, amount % v.shape[axis], axis)

    def inplane(v, dz, dy):
        up_z = jnp.where(z < edge - dz, roll(v, -dz, 2), 0.0)
        down_z = jnp.where(z >= dz, roll(v, dz, 2), 0.0)
        ru = roll(v, -dy, 2)
        up_y = jnp.where(lane < LANES - dy, ru, roll(ru, -1, 1))
        rd = roll(v, dy, 2)
        down_y = jnp.where(lane >= dy, rd, roll(rd, 1, 1))
        return (up_z + down_z) + (up_y + down_y)

    def load(ref, p, n):
        return ref[pl.ds((p + 1) * SUBS, n * SUBS), :].reshape(n, SUBS, LANES)

    def store(ref, p, value):
        n = value.shape[0]
        ref[pl.ds((p + 1) * SUBS, n * SUBS), :] = value.reshape(n * SUBS, LANES)

    def lap(ref, p, n, dz=1, dy=edge):
        wide = load(ref, p - 1, n + 2)
        v = wide[1:-1]
        return v, 6.0 * v - (wide[:-2] + wide[2:]) - inplane(v, dz, dy)

    def slot_mask(s):
        return mask[pl.ds(SUBS * s, SUBS), :][None]

    chunk = SUBS
    per_slot = edge // chunk
    chunks = (slots + 2) * per_slot

    def vcycle(result):
        for c in range(chunks):
            r, applied = lap(rhs, c * chunk, chunk)
            store(smooth, c * chunk, slot_mask(c // per_slot) * (2.0 * step * r - step * step * applied))
        for c in range(chunks):
            v, applied = lap(smooth, c * chunk, chunk)
            q = load(rhs, c * chunk, chunk) - applied
            q = q.reshape(chunk // 2, 2, SUBS, LANES)
            q = q[:, 0] + q[:, 1]
            q = q + jnp.where(lane % 2 == 0, roll(q, -1, 2), roll(q, 1, 2))
            q = q + jnp.where(lane // edge % 2 == 0, roll(q, -edge, 2), roll(q, edge, 2))
            store(coarse, c * chunk // 2, slot_mask(c // per_slot) * (0.125 * q))
        half = edge // 2
        for s in range(slots + 2):
            v, applied = lap(coarse, s * half, half, 2, 2 * edge)
            store(ea, s * half, slot_mask(s) * (2.0 * cstep * v - 0.25 * cstep * cstep * applied))
        now, then = ea, eb
        for sweep in range(COARSE_SWEEPS - 2):
            for s in range(slots + 2):
                v, applied = lap(now, s * half, half, 2, 2 * edge)
                c = load(coarse, s * half, half)
                value = slot_mask(s) * (v + cstep * (c - 0.25 * applied))
                store(then, s * half, value)
            now, then = then, now
        for c in range(1, chunks - 1):
            e = load(now, c * chunk // 2, chunk // 2)[:, None]
            e = jnp.broadcast_to(e, (chunk // 2, 2, SUBS, LANES)).reshape(chunk, SUBS, LANES)
            store(smooth, c * chunk, load(smooth, c * chunk, chunk) + e)
        now, then = smooth, other
        for sweep in range(POST_SWEEPS):
            for c in range(1, chunks - 1):
                v, applied = lap(now, c * chunk, chunk)
                r = load(rhs, c * chunk, chunk)
                store(then, c * chunk, slot_mask(c // per_slot) * (v + step * (r - applied)))
            now, then = then, now
        return now

    def natural(ref, s, h, t):
        plane = 1 + (s + 1) * edge + h * SUBS
        return ref[pl.ds(plane * SUBS + middle + t, SUBS, stride=SUBS), :]

    def owned_tiles():
        for s in range(slots):
            for h in range(edge // SUBS):
                for t in range(tiles):
                    yield s, h, t, pl.ds(s * edge + h * SUBS, SUBS), pl.ds(t * LANES, LANES)

    pick_last(0, source_ref)
    pl.semaphore_wait(barrier, n_grp - 1 + n_sfc - 1 + diagonals)
    start(0, source_ref)
    receive(0, source_ref)
    unpack(0, source_ref)
    z0 = vcycle(None)
    for c in range(per_slot, chunks - per_slot):
        _, applied = lap(z0, c * chunk, chunk)
        store(other, c * chunk, applied)
    acc_rz = jnp.zeros((SUBS, LANES), jnp.float32)
    acc_curv = jnp.zeros((SUBS, LANES), jnp.float32)
    for s, h, t, rows, cols in owned_tiles():
        value = natural(z0, s, h, t)
        image = natural(other, s, h, t)
        source = source_ref[rows, cols]
        if s:
            value = jnp.where(count > s, value, 0.0)
            image = jnp.where(count > s, image, 0.0)
            source = jnp.where(count > s, source, 0.0)
        first_ref[rows, cols] = value
        image_ref[rows, cols] = image
        acc_rz = acc_rz + source * value
        acc_curv = acc_curv + value * image
    pick_last(1, image_ref)
    start(1, image_ref)
    receive(1, image_ref)
    unpack(1, image_ref)
    w = vcycle(None)
    acc_s = jnp.zeros((SUBS, LANES), jnp.float32)
    for s, h, t, rows, cols in owned_tiles():
        value = natural(w, s, h, t)
        if s:
            value = jnp.where(count > s, value, 0.0)
        direction_ref[rows, cols] = value
        acc_s = acc_s + value * image_ref[rows, cols]

    sums = [jnp.sum(a, axis=0, keepdims=True) for a in (acc_rz, acc_curv, acc_s)]
    sums = sums + [jnp.zeros((SUBS - 3, LANES), jnp.float32)]
    part[...] = jnp.concatenate(sums, axis=0)

    def reduce(src, dst, axis, size, me, send, recv):
        def copy(slot, target):
            return pltpu.make_async_remote_copy(
                src_ref=src, dst_ref=dst.at[slot], send_sem=send.at[target],
                recv_sem=recv.at[slot], device_id={axis: target}, device_id_type=MESH,
            )

        def go(i, carry):
            copy(me, lax.rem(me + i, size)).start()
            return carry

        lax.fori_loop(1, size, go, 0)
        dst[me] = src[...]

        def got(i, carry):
            j = lax.rem(me + i, size)
            copy(j, j).wait_recv()
            return carry

        lax.fori_loop(1, size, got, 0)

        def add(i, acc):
            return acc + dst[i]

        return lax.fori_loop(0, size, add, jnp.zeros((SUBS, LANES), jnp.float32))

    def done(src, dst, axis, size, me, send, recv):
        def out(i, carry):
            j = lax.rem(me + i, size)
            pltpu.make_async_remote_copy(
                src_ref=src, dst_ref=dst.at[me], send_sem=send.at[j],
                recv_sem=recv.at[me], device_id={axis: j}, device_id_type=MESH,
            ).wait_send()
            return carry

        lax.fori_loop(1, size, out, 0)

    by_grp = (part, red_grp, "grp", n_grp, grp, grp_send, grp_recv)
    by_sfc = (total, red_sfc, "sfc", n_sfc, sfc, sfc_send, sfc_recv)
    total[...] = reduce(*by_grp)
    grand = jnp.sum(reduce(*by_sfc), axis=1, keepdims=True)
    rz, curv, cross = grand[0:1], grand[1:2], grand[2:3]
    alpha = rz / curv
    ratio = cross / curv
    for s, h, t, rows, cols in owned_tiles():
        source = source_ref[rows, cols]
        if s:
            source = jnp.where(count > s, source, 0.0)
        first = first_ref[rows, cols]
        solution_ref[rows, cols] = alpha * first
        residual_ref[rows, cols] = source - alpha * image_ref[rows, cols]
        direction_ref[rows, cols] = alpha * (ratio * first - direction_ref[rows, cols])
    sent(0, source_ref)
    sent(1, image_ref)
    done(*by_grp)
    done(*by_sfc)


def shards(n_sfc, n_grp, source, layer_counts):
    slots, edge, width = source.shape
    planes, tiles = slots * edge, width // LANES
    padded = (planes + 2 * edge + 2) * SUBS
    half_padded = ((slots + 2) * edge // 2 + 2) * SUBS
    f32 = jnp.float32
    vmem = pltpu.VMEM
    dma = pltpu.SemaphoreType.DMA
    out = jax.ShapeDtypeStruct((planes, width), f32)
    outs = pl.pallas_call(
        functools.partial(kernel, (slots, edge, tiles, n_sfc, n_grp)),
        out_shape=(out, out, out),
        in_specs=[
            pl.BlockSpec(memory_space=pltpu.SMEM),
            pl.BlockSpec(memory_space=pltpu.VMEM),
        ],
        out_specs=[pl.BlockSpec(memory_space=pltpu.VMEM)] * 3,
        scratch_shapes=[
            vmem((padded, LANES), f32),
            vmem((padded, LANES), f32),
            vmem((padded, LANES), f32),
            vmem((half_padded, LANES), f32),
            vmem((half_padded, LANES), f32),
            vmem((half_padded, LANES), f32),
            vmem(((slots + 2) * SUBS, LANES), f32),
            vmem((planes, width), f32),
            vmem((planes, width), f32),
            vmem((2, edge, width), f32),
            vmem((2, 2, planes, width), f32),
            vmem((2, 3, edge, width), f32),
            vmem((2, 3, edge, width), f32),
            vmem((SUBS, LANES), f32),
            vmem((SUBS, LANES), f32),
            vmem((n_grp, SUBS, LANES), f32),
            vmem((n_sfc, SUBS, LANES), f32),
            dma((2, len(WAYS))),
            dma((2, len(WAYS))),
            dma((n_grp,)),
            dma((n_grp,)),
            dma((n_sfc,)),
            dma((n_sfc,)),
        ],
        compiler_params=pltpu.CompilerParams(collective_id=0, has_side_effects=True),
        name="pcg",
    )(layer_counts, source.reshape(planes, width))
    return tuple(o.reshape(source.shape) for o in outs)


def solution(mesh):
    n_sfc, n_grp = mesh.shape["sfc"], mesh.shape["grp"]
    return jax.shard_map(
        functools.partial(shards, n_sfc, n_grp),
        mesh=mesh,
        in_specs=(P("sfc", None, "grp"), P("sfc")),
        out_specs=(P("sfc", None, "grp"), P("sfc", None, "grp"), P("sfc", None, "grp")),
        check_vma=False,
    )
```

time: 300 us -> 34.5 us (0.12)
  starting transfers between devices: 120 us -> 0 us
  blocking collectives: 89.4 us -> 0 us
  waiting for transfers between devices: 42.4 us -> 0 us
  Pallas kernels: 0 us -> 29.9 us
  local copies, waits for them, and re-layouts: 28.7 us -> 3 us
  other arithmetic: 13.1 us -> 0 us
  between operations: 5.23 us -> 1.3 us
    ppermute x44 -> x0, starting transfers between devices: 120 us -> none  [the longest x22 91.2 us: padded_2(): lax.ppermute(tail, axis, [(i, (i + 1) % count) for i in range(ends)])]
    psum x2 -> x0, blocking collectives: 89.4 us -> none  [the longest x1 45.1 us: shards(): rz_value = lax.psum(jnp.sum(first_rhs * first_z), ('sfc', 'grp'))]
    ppermute x44 -> x0, waiting for transfers between devices: 42.4 us -> none  [the longest x22 32.1 us: padded_2(): lax.ppermute(head, axis, [((i + 1) % count, i) for i in range(ends)])]
    pallas_call x0 -> x1, Pallas kernels: none -> 29.9 us  [shards(): pl.pallas_call(functools.partial(kernel, (slots, edge, tiles, n_sfc, n_gr...]
    reshape x4 -> x0, local copies, waits for them, and re-layouts: 19.3 us -> none  [the longest x2 11.2 us: restrict(): blocks = field.reshape(planes // 2, 2, half, 2, half, 2)]
    reduce_sum x4 -> x0, other arithmetic: 6.74 us -> none  [the longest x2 5.2 us: restrict(): jnp.sum(blocks, axis=(1, 3, 5)).reshape(planes // 2, half * half)]
    broadcast_in_dim x4 -> x0, local copies, waits for them, and re-layouts: 4.98 us -> none  [prolong(): blocks = jnp.broadcast_to(blocks, (planes, 2, half, 2, half, 2))]
    slice x72 -> x0, local copies, waits for them, and re-layouts: 3.72 us -> none  [the longest x8 0.73 us: padded_laplace(): field[:, 1:]]
  transfers between devices with their start and end apart: 44 -> 0, of which waited for: 15 -> 0; matrix products, arithmetic and copies ran while one was open for 1% -> 0% of each run, Pallas kernels for 0% -> 0%
where the time goes in v1:
time: 34.5 us; the launch traced here: 34.2 us
  Pallas kernels  29.9 us (87%)
  local copies, waits for them, and re-layouts  3 us (9%)
  between operations  1.3 us (4%)
    pallas_call x1, Pallas kernels, shards(): pl.pallas_call(functools.partial(kernel, (slots, edge, tiles, n_sfc, n_gr...  29.9 us
    unnamed x7, local copies, waits for them, and re-layouts  3 us

profile of v1, /device:TPU:0, one launch (start us, length us, event | category | flops | bytes accessed | tf_op | source)
XLA Modules:
  0.0 34.2 jit_solution(18025601643885198508)
XLA Ops:
  1.3 29.9 %pcg.1 = (f32[64,256]{1,0:T(8,128)}, f32[64,256]{1,0:T(8,128)}, f32[64,256]{1,0:T(8,128)}) custom-call(s32[1]{0:T(128)S(6)} %copy.8.count_ref, f32[64,256]{1,0:T(8,128)} %bitcast.4), custom_call_target="tpu_custom_call" | custom-call | tf_op jit(solution)/shard_map/pcg/pallas_call | solution.py:358
  31.2 0.0 copy-start.1
  31.2 1.5 %copy.9 = f32[4,16,256]{2,1,0:T(8,128)} copy(f32[4,16,256]{2,1,0:T(8,128)} %bitcast.7) | data formatting | bytes 131072
  32.7 0.0 copy-done.1
  32.7 0.0 copy-start
  32.7 0.6 %copy.10 = f32[4,16,256]{2,1,0:T(8,128)} copy(f32[4,16,256]{2,1,0:T(8,128)S(1)} %bitcast.6) | data formatting | bytes 131072
  33.3 0.2 copy-done
  33.6 0.6 %copy.11 = f32[4,16,256]{2,1,0:T(8,128)} copy(f32[4,16,256]{2,1,0:T(8,128)S(1)} %bitcast.5) | data formatting | bytes 131072
Async XLA Ops:
  31.2 1.5 %copy-start.1 = (f32[64,256]{1,0:T(8,128)S(1)}, f32[64,256]{1,0:T(8,128)}, u32[]{:S(2)}) copy-start(f32[64,256]{1,0:T(8,128)} %get-tuple-element.7) | copy-start | bytes 196612
  32.7 0.9 %copy-start = (f32[64,256]{1,0:T(8,128)S(1)}, f32[64,256]{1,0:T(8,128)}, u32[]{:S(2)}) copy-start(f32[64,256]{1,0:T(8,128)} %get-tuple-element.8) | copy-start | bytes 196612

commit v2 on v1

--- a/solution.py
+++ b/solution.py
@@ -17,16 +17,17 @@
 
 
 def kernel(
-    dims, count_ref, source_ref, solution_ref, residual_ref, direction_ref,
-    rhs, smooth, other, coarse, ea, eb, mask, image_ref, first_ref, last,
-    side, below, above, part, total, red_grp, red_sfc,
-    send_sem, recv_sem, grp_send, grp_recv, sfc_send, sfc_recv,
+    dims, count_hbm, source_hbm, first_ref, image_ref, w_ref, source_out, scale_ref,
+    source_ref, image_buf, counts, rhs, smooth, other, coarse, ea, eb, mask, own, last,
+    side, below, above, part, red, local_sem,
+    send_sem, recv_sem, red_send, red_recv,
 ):
     slots, edge, tiles, n_sfc, n_grp = dims
     planes = slots * edge
     sfc = lax.axis_index("sfc")
     grp = lax.axis_index("grp")
-    count = count_ref[0]
+    me = sfc * n_grp + grp
+    everyone = n_sfc * n_grp
     step = OMEGA / 6.0
     cstep = OMEGA / 1.5
     middle = (SUBS - tiles) // 2
@@ -42,32 +43,22 @@
 
     barrier = pltpu.get_barrier_semaphore()
 
-    def greet(i, axis, size, me):
-        pl.semaphore_signal(
-            barrier, inc=1, device_id={axis: lax.rem(me + i, size)}, device_id_type=MESH
-        )
-
-    for i in range(1, n_grp):
-        greet(i, "grp", n_grp, grp)
-
-    def greet_sfc(i, carry):
-        greet(i, "sfc", n_sfc, sfc)
+    def place(i):
+        peer = lax.rem(me + i, everyone)
+        return peer, {"sfc": peer // n_grp, "grp": lax.rem(peer, n_grp)}
+
+    def greet(i, carry):
+        pl.semaphore_signal(barrier, inc=1, device_id=place(i)[1], device_id_type=MESH)
         return carry
 
-    lax.fori_loop(1, n_sfc, greet_sfc, 0)
-    for ds, dg in WAYS:
-        if ds and dg:
-            @pl.when(there(ds, dg))
-            def _():
-                pl.semaphore_signal(
-                    barrier, inc=1, device_id={"sfc": sfc + ds, "grp": grp + dg},
-                    device_id_type=MESH,
-                )
+    count_copy = pltpu.make_async_copy(count_hbm, counts, local_sem.at[0])
+    source_copy = pltpu.make_async_copy(source_hbm, source_ref, local_sem.at[1])
+    count_copy.start()
+    source_copy.start()
+    lax.fori_loop(1, everyone, greet, 0)
 
     def one(flag):
         return jnp.where(flag, 1, 0)
-
-    diagonals = (one(sfc > 0) + one(sfc < n_sfc - 1)) * (one(grp > 0) + one(grp < n_grp - 1))
 
     lane = lax.broadcasted_iota(jnp.int32, (1, SUBS, LANES), 2)
     sub = lax.broadcasted_iota(jnp.int32, (1, SUBS, LANES), 1)
@@ -87,6 +78,14 @@
         jnp.where(owned, 1, 0) + jnp.where(lefts, 1, 0) * has_left
         + jnp.where(rights, 1, 0) * has_right
     )
+    def zero_rhs(i, carry):
+        rhs[pl.ds(i * SUBS, SUBS), :] = jnp.zeros((SUBS, LANES), jnp.float32)
+        return carry
+
+    lax.fori_loop(0, planes + 2 * edge + 2, zero_rhs, 0)
+
+    count_copy.wait()
+    count = counts[0]
     for s in range(slots + 2):
         if s == 0:
             ok = has_below
@@ -94,17 +93,9 @@
             ok = one(count >= s) + one(count == s - 1) * has_above
         mask[pl.ds(SUBS * s, SUBS), :] = (rows_ok * ok).astype(jnp.float32)[0]
 
-    def zero_rhs(i, carry):
-        rhs[pl.ds(i * SUBS, SUBS), :] = jnp.zeros((SUBS, LANES), jnp.float32)
-        return carry
-
-    lax.fori_loop(0, planes + 2 * edge + 2, zero_rhs, 0)
-
-    def fill_last(src):
-        value = src[pl.ds(0, edge), :]
-        for s in range(1, slots):
-            value = jnp.where(count > s, src[pl.ds(s * edge, edge), :], value)
-        last[...] = value
+    for s in range(slots):
+        mine = jnp.where(owned, 1, 0) * one(count > s)
+        own[pl.ds(SUBS * s, SUBS), :] = mine.astype(jnp.float32)[0]
 
     def copies(e, i, ds, dg, src):
         gpos = 1 - dg
@@ -201,13 +192,18 @@
     per_slot = edge // chunk
     chunks = (slots + 2) * per_slot
 
-    def vcycle(result):
+    def vcycle(on_sum=None):
+        acc = jnp.zeros((SUBS, LANES), jnp.float32)
         for c in range(chunks):
             r, applied = lap(rhs, c * chunk, chunk)
             store(smooth, c * chunk, slot_mask(c // per_slot) * (2.0 * step * r - step * step * applied))
         for c in range(chunks):
             v, applied = lap(smooth, c * chunk, chunk)
-            q = load(rhs, c * chunk, chunk) - applied
+            r = load(rhs, c * chunk, chunk)
+            q = r - applied
+            s = c // per_slot - 1
+            if on_sum is not None and 0 <= s < slots:
+                acc = acc + own[pl.ds(SUBS * s, SUBS), :] * jnp.sum((r + q) * v, axis=0)
             q = q.reshape(chunk // 2, 2, SUBS, LANES)
             q = q[:, 0] + q[:, 1]
             q = q + jnp.where(lane % 2 == 0, roll(q, -1, 2), roll(q, 1, 2))
@@ -225,6 +221,11 @@
                 value = slot_mask(s) * (v + cstep * (c - 0.25 * applied))
                 store(then, s * half, value)
             now, then = then, now
+        if on_sum is not None:
+            for s in range(slots):
+                ce = load(coarse, (s + 1) * half, half) * load(now, (s + 1) * half, half)
+                acc = acc + own[pl.ds(SUBS * s, SUBS), :] * (2.0 * jnp.sum(ce, axis=0))
+            on_sum(acc)
         for c in range(1, chunks - 1):
             e = load(now, c * chunk // 2, chunk // 2)[:, None]
             e = jnp.broadcast_to(e, (chunk // 2, 2, SUBS, LANES)).reshape(chunk, SUBS, LANES)
@@ -248,12 +249,13 @@
                 for t in range(tiles):
                     yield s, h, t, pl.ds(s * edge + h * SUBS, SUBS), pl.ds(t * LANES, LANES)
 
+    source_copy.wait()
     pick_last(0, source_ref)
-    pl.semaphore_wait(barrier, n_grp - 1 + n_sfc - 1 + diagonals)
+    pl.semaphore_wait(barrier, everyone - 1)
     start(0, source_ref)
     receive(0, source_ref)
     unpack(0, source_ref)
-    z0 = vcycle(None)
+    z0 = vcycle()
     for c in range(per_slot, chunks - per_slot):
         _, applied = lap(z0, c * chunk, chunk)
         store(other, c * chunk, applied)
@@ -269,81 +271,80 @@
             source = jnp.where(count > s, source, 0.0)
         first_ref[rows, cols] = value
         image_ref[rows, cols] = image
+        image_buf[rows, cols] = image
+        source_out[rows, cols] = source
         acc_rz = acc_rz + source * value
         acc_curv = acc_curv + value * image
-    pick_last(1, image_ref)
-    start(1, image_ref)
-    receive(1, image_ref)
-    unpack(1, image_ref)
-    w = vcycle(None)
-    acc_s = jnp.zeros((SUBS, LANES), jnp.float32)
+    pick_last(1, image_buf)
+    start(1, image_buf)
+    row = lax.broadcasted_iota(jnp.int32, (1, LANES), 1)
+
+    def whole(acc):
+        return jnp.sum(jnp.sum(acc, axis=0, keepdims=True), axis=1, keepdims=True)
+
+    rz, curv = whole(acc_rz), whole(acc_curv)
+    known = jnp.where(row == 0, rz, jnp.where(row == 1, curv, 0.0))
+    receive(1, image_buf)
+    unpack(1, image_buf)
+
+    def send(slot, peer, device):
+        return pltpu.make_async_remote_copy(
+            src_ref=part, dst_ref=red.at[slot], send_sem=red_send.at[peer],
+            recv_sem=red_recv.at[slot], device_id=device, device_id_type=MESH,
+        )
+
+    def spread(acc):
+        value = jnp.where(row == 2, whole(acc), known)
+        part[...] = value
+        red[me] = value
+
+        def go(i, carry):
+            peer, device = place(i)
+            send(me, peer, device).start()
+            return carry
+
+        lax.fori_loop(1, everyone, go, 0)
+
+    w = vcycle(spread)
     for s, h, t, rows, cols in owned_tiles():
         value = natural(w, s, h, t)
         if s:
             value = jnp.where(count > s, value, 0.0)
-        direction_ref[rows, cols] = value
-        acc_s = acc_s + value * image_ref[rows, cols]
-
-    sums = [jnp.sum(a, axis=0, keepdims=True) for a in (acc_rz, acc_curv, acc_s)]
-    sums = sums + [jnp.zeros((SUBS - 3, LANES), jnp.float32)]
-    part[...] = jnp.concatenate(sums, axis=0)
-
-    def reduce(src, dst, axis, size, me, send, recv):
-        def copy(slot, target):
-            return pltpu.make_async_remote_copy(
-                src_ref=src, dst_ref=dst.at[slot], send_sem=send.at[target],
-                recv_sem=recv.at[slot], device_id={axis: target}, device_id_type=MESH,
-            )
-
-        def go(i, carry):
-            copy(me, lax.rem(me + i, size)).start()
-            return carry
-
-        lax.fori_loop(1, size, go, 0)
-        dst[me] = src[...]
-
-        def got(i, carry):
-            j = lax.rem(me + i, size)
-            copy(j, j).wait_recv()
-            return carry
-
-        lax.fori_loop(1, size, got, 0)
-
-        def add(i, acc):
-            return acc + dst[i]
-
-        return lax.fori_loop(0, size, add, jnp.zeros((SUBS, LANES), jnp.float32))
-
-    def done(src, dst, axis, size, me, send, recv):
-        def out(i, carry):
-            j = lax.rem(me + i, size)
-            pltpu.make_async_remote_copy(
-                src_ref=src, dst_ref=dst.at[me], send_sem=send.at[j],
-                recv_sem=recv.at[me], device_id={axis: j}, device_id_type=MESH,
-            ).wait_send()
-            return carry
-
-        lax.fori_loop(1, size, out, 0)
-
-    by_grp = (part, red_grp, "grp", n_grp, grp, grp_send, grp_recv)
-    by_sfc = (total, red_sfc, "sfc", n_sfc, sfc, sfc_send, sfc_recv)
-    total[...] = reduce(*by_grp)
-    grand = jnp.sum(reduce(*by_sfc), axis=1, keepdims=True)
-    rz, curv, cross = grand[0:1], grand[1:2], grand[2:3]
-    alpha = rz / curv
-    ratio = cross / curv
-    for s, h, t, rows, cols in owned_tiles():
-        source = source_ref[rows, cols]
-        if s:
-            source = jnp.where(count > s, source, 0.0)
-        first = first_ref[rows, cols]
-        solution_ref[rows, cols] = alpha * first
-        residual_ref[rows, cols] = source - alpha * image_ref[rows, cols]
-        direction_ref[rows, cols] = alpha * (ratio * first - direction_ref[rows, cols])
+        w_ref[rows, cols] = value
     sent(0, source_ref)
-    sent(1, image_ref)
-    done(*by_grp)
-    done(*by_sfc)
+    sent(1, image_buf)
+
+    def got(i, carry):
+        peer, device = place(i)
+        send(peer, peer, device).wait_recv()
+        return carry
+
+    lax.fori_loop(1, everyone, got, 0)
+    sums = jnp.sum(red[...], axis=0)
+
+    def pick(i):
+        return jnp.sum(jnp.where(row == i, sums, 0.0), axis=1, keepdims=True)
+
+    alpha = pick(0) / pick(1)
+    ratio = pick(2) / pick(1)
+    scale_ref[...] = jnp.concatenate(
+        [jnp.broadcast_to(alpha, (1, LANES)), jnp.broadcast_to(ratio, (1, LANES))], axis=0
+    )
+
+    def out(i, carry):
+        peer, device = place(i)
+        send(me, peer, device).wait_send()
+        return carry
+
+    lax.fori_loop(1, everyone, out, 0)
+
+
+def combine(first, image, w, source, scale, solution_ref, residual_ref, direction_ref):
+    alpha = scale[0:1, 0:1]
+    ratio = scale[1:2, 0:1]
+    solution_ref[...] = alpha * first[...]
+    residual_ref[...] = source[...] - alpha * image[...]
+    direction_ref[...] = alpha * (ratio * first[...] - w[...])
 
 
 def shards(n_sfc, n_grp, source, layer_counts):
@@ -354,16 +355,17 @@
     f32 = jnp.float32
     vmem = pltpu.VMEM
     dma = pltpu.SemaphoreType.DMA
+    n = n_sfc * n_grp
     out = jax.ShapeDtypeStruct((planes, width), f32)
-    outs = pl.pallas_call(
+    parts = pl.pallas_call(
         functools.partial(kernel, (slots, edge, tiles, n_sfc, n_grp)),
-        out_shape=(out, out, out),
-        in_specs=[
-            pl.BlockSpec(memory_space=pltpu.SMEM),
-            pl.BlockSpec(memory_space=pltpu.VMEM),
-        ],
-        out_specs=[pl.BlockSpec(memory_space=pltpu.VMEM)] * 3,
+        out_shape=(out, out, out, out, jax.ShapeDtypeStruct((2, LANES), f32)),
+        in_specs=[pl.BlockSpec(memory_space=pl.ANY)] * 2,
+        out_specs=[pl.BlockSpec(memory_space=pltpu.VMEM)] * 5,
         scratch_shapes=[
+            vmem((planes, width), f32),
+            vmem((planes, width), f32),
+            pltpu.SMEM((1,), jnp.int32),
             vmem((padded, LANES), f32),
             vmem((padded, LANES), f32),
             vmem((padded, LANES), f32),
@@ -371,26 +373,32 @@
             vmem((half_padded, LANES), f32),
             vmem((half_padded, LANES), f32),
             vmem(((slots + 2) * SUBS, LANES), f32),
-            vmem((planes, width), f32),
-            vmem((planes, width), f32),
+            vmem((slots * SUBS, LANES), f32),
             vmem((2, edge, width), f32),
             vmem((2, 2, planes, width), f32),
             vmem((2, 3, edge, width), f32),
             vmem((2, 3, edge, width), f32),
-            vmem((SUBS, LANES), f32),
-            vmem((SUBS, LANES), f32),
-            vmem((n_grp, SUBS, LANES), f32),
-            vmem((n_sfc, SUBS, LANES), f32),
+            vmem((1, LANES), f32),
+            vmem((n, 1, LANES), f32),
+            dma((2,)),
             dma((2, len(WAYS))),
             dma((2, len(WAYS))),
-            dma((n_grp,)),
-            dma((n_grp,)),
-            dma((n_sfc,)),
-            dma((n_sfc,)),
+            dma((n,)),
+            dma((n,)),
         ],
-        compiler_params=pltpu.CompilerParams(collective_id=0, has_side_effects=True),
+        compiler_params=pltpu.CompilerParams(
+            collective_id=0, has_side_effects=True, vmem_limit_bytes=16 * 1024 * 1024
+        ),
         name="pcg",
     )(layer_counts, source.reshape(planes, width))
+    outs = pl.pallas_call(
+        combine,
+        out_shape=(out, out, out),
+        in_specs=[pl.BlockSpec(memory_space=pltpu.VMEM)] * 5,
+        out_specs=[pl.BlockSpec(memory_space=pltpu.VMEM)] * 3,
+        compiler_params=pltpu.CompilerParams(vmem_limit_bytes=16 * 1024 * 1024),
+        name="combine",
+    )(*parts)
     return tuple(o.reshape(source.shape) for o in outs)
 
 

time: 34.5 us -> 29.9 us (0.87)
  Pallas kernels: 29.9 us -> 27.6 us
  local copies, waits for them, and re-layouts: 3 us -> 0.83 us
    pallas_call x1, Pallas kernels: 29.9 us -> 26.8 us  [shards(): pl.pallas_call(functools.partial(kernel, (slots, edge, tiles, n_sfc, n_gr...]
    unnamed x7 -> x2, local copies, waits for them, and re-layouts: 3 us -> 0.83 us
    pallas_call x0 -> x1, Pallas kernels: none -> 0.72 us  [shards(): pl.pallas_call(combine, out_shape=(out, out, out), in_specs=[pl.BlockSpec...]
where the time goes in v2:
time: 29.9 us; the launch traced here: 29.7 us
  Pallas kernels  27.6 us (92%)
  between operations  1.29 us (4%)
  local copies, waits for them, and re-layouts  0.83 us (3%)
    pallas_call x1, Pallas kernels, shards(): pl.pallas_call(functools.partial(kernel, (slots, edge, tiles, n_sfc, n_gr...  26.8 us
    unnamed x2, local copies, waits for them, and re-layouts  0.83 us
    pallas_call x1, Pallas kernels, shards(): pl.pallas_call(combine, out_shape=(out, out, out), in_specs=[pl.BlockSpec...  0.72 us

profile of v2, /device:TPU:0, one launch (start us, length us, event | category | flops | bytes accessed | tf_op | source)
XLA Modules:
  0.0 29.7 jit_solution(12402360788004943912)
XLA Ops:
  1.3 0.0 copy-start
  1.3 0.8 %copy-done = f32[4,16,256]{2,1,0:T(8,128)S(1)} copy-done((f32[4,16,256]{2,1,0:T(8,128)S(1)}, f32[4,16,256]{2,1,0:T(8,128)}, u32[]{:S(2)}) %copy-start) | copy-done | bytes 65560
  2.1 26.8 %pcg.1 = (f32[64,256]{1,0:T(8,128)S(1)}, f32[64,256]{1,0:T(8,128)S(1)}, f32[64,256]{1,0:T(8,128)S(1)}, f32[64,256]{1,0:T(8,128)S(1)}, f32[2,128]{1,0:T(2,128)S(1)}) custom-call(s32[1]{0:T(128)S(6)} %copy.5.count_hbm, f32[64,256]{1,0:T(8,128)S(1)} %bitcast.4), custom_call_target="tpu_custom_call" | custom-call | tf_op jit(solution)/shard_map/pcg/pallas_call | solution.py:360
  29.0 0.7 %combine.1 = (f32[64,256]{1,0:T(8,128)}, f32[64,256]{1,0:T(8,128)}, f32[64,256]{1,0:T(8,128)}) custom-call(f32[64,256]{1,0:T(8,128)S(1)} %get-tuple-element.11.first, f32[64,256]{1,0:T(8,128)S(1)} %get-tuple-element.12.image, f32[64,256]{1,0:T(8,128)S(1)} %get-tuple-element.13.w, f32[64,256]{1,0:T(8,128)S(1)} %get-tuple-element.14.source, ...), custom_call_target="tpu_custom_call" | custom-call | tf_op jit(solution)/shard_map/combine/pallas_call | solution.py:394
Async XLA Ops:
  1.3 0.8 %copy-start = (f32[4,16,256]{2,1,0:T(8,128)S(1)}, f32[4,16,256]{2,1,0:T(8,128)}, u32[]{:S(2)}) copy-start(f32[4,16,256]{2,1,0:T(8,128)} %param.2) | copy-start | bytes 196612

commit v3 on v2

--- a/solution.py
+++ b/solution.py
@@ -18,9 +18,9 @@
 
 def kernel(
     dims, count_hbm, source_hbm, first_ref, image_ref, w_ref, source_out, scale_ref,
-    source_ref, image_buf, counts, rhs, smooth, other, coarse, ea, eb, mask, own, last,
+    source_ref, image_buf, counts, rhs, smooth, other, coarse, ea, eb, mask, own, packed,
     side, below, above, part, red, local_sem,
-    send_sem, recv_sem, red_send, red_recv,
+    send_sem, recv_sem, red_send, red_recv, hello,
 ):
     slots, edge, tiles, n_sfc, n_grp = dims
     planes = slots * edge
@@ -41,6 +41,7 @@
             flag = extra if flag is None else jnp.logical_and(flag, extra)
         return flag
 
+    gossip = n_sfc <= 9 and n_grp <= 4
     barrier = pltpu.get_barrier_semaphore()
 
     def place(i):
@@ -55,10 +56,32 @@
     source_copy = pltpu.make_async_copy(source_hbm, source_ref, local_sem.at[1])
     count_copy.start()
     source_copy.start()
-    lax.fori_loop(1, everyone, greet, 0)
+    if gossip:
+        for ds, dg in WAYS:
+            @pl.when(there(ds, dg))
+            def _(ds=ds, dg=dg):
+                pl.semaphore_signal(
+                    barrier, inc=1, device_id={"sfc": sfc + ds, "grp": grp + dg},
+                    device_id_type=MESH,
+                )
+    else:
+        lax.fori_loop(1, everyone, greet, 0)
 
     def one(flag):
         return jnp.where(flag, 1, 0)
+
+    def greet_far(rnd, far):
+        if gossip and far < n_sfc:
+            for ds in (far, -far):
+                @pl.when(sfc + ds < n_sfc if ds > 0 else sfc + ds >= 0)
+                def _(ds=ds):
+                    pl.semaphore_signal(
+                        hello.at[rnd], inc=1, device_id={"sfc": sfc + ds}, device_id_type=MESH
+                    )
+
+    def hear_far(rnd, far):
+        if gossip and far < n_sfc:
+            pl.semaphore_wait(hello.at[rnd], one(sfc + far < n_sfc) + one(sfc >= far))
 
     lane = lax.broadcasted_iota(jnp.int32, (1, SUBS, LANES), 2)
     sub = lax.broadcasted_iota(jnp.int32, (1, SUBS, LANES), 1)
@@ -101,10 +124,10 @@
         gpos = 1 - dg
         if ds == 0:
             source, target = src, side.at[e, gpos // 2]
-        elif ds > 0:
-            source, target = last.at[e], below.at[e, gpos]
         else:
-            source, target = src.at[pl.ds(0, edge)], above.at[e, gpos]
+            tile, amount = ((0, 2), (1, 3), (3, 2))[dg + 1]
+            source = packed.at[e, int(ds > 0), pl.ds(tile, amount)]
+            target = (below if ds > 0 else above).at[e, gpos, pl.ds(0, amount)]
         return pltpu.make_async_remote_copy(
             src_ref=source, dst_ref=target, send_sem=send_sem.at[e, i],
             recv_sem=recv_sem.at[e, i], device_id={"sfc": sfc + ds, "grp": grp + dg},
@@ -129,11 +152,53 @@
             def _(i=i, ds=ds, dg=dg):
                 copies(e, i, ds, dg, src).wait_send()
 
-    def pick_last(e, src):
-        value = src[pl.ds(0, edge), :]
-        for s in range(1, slots):
-            value = jnp.where(count > s, src[pl.ds(s * edge, edge), :], value)
-        last[e] = value
+    def pack(e, src):
+        cut = SUBS // 2
+        for up in (0, 1):
+            rows = pl.ds(0, edge)
+            value = [src[rows, pl.ds(t * LANES, LANES)] for t in range(tiles)]
+            if up:
+                for s in range(1, slots):
+                    rows = pl.ds(s * edge, edge)
+                    value = [
+                        jnp.where(count > s, src[rows, pl.ds(t * LANES, LANES)], value[t])
+                        for t in range(tiles)
+                    ]
+            if up:
+                near = [v[edge - SUBS :] for v in value]
+                far = [v[edge - SUBS - cut : edge - SUBS] for v in value]
+                edges = [v[edge - cut :] for v in value]
+            else:
+                near = [v[:SUBS] for v in value]
+                far = [v[SUBS : SUBS + cut] for v in value]
+                edges = [v[:cut] for v in value]
+            packed[e, up, 0] = jnp.concatenate([far[0], edges[1]], axis=0)
+            packed[e, up, 1] = near[0]
+            packed[e, up, 2] = jnp.concatenate([far[0], far[1]], axis=0)
+            packed[e, up, 3] = near[1]
+            packed[e, up, 4] = jnp.concatenate([far[1], edges[0]], axis=0)
+
+    def ghost(ref, e, up, g, h, t):
+        cut = SUBS // 2
+        near_h = 1 if up else 0
+        if g == 1:
+            if h == near_h:
+                return ref[e, g, 0 if t == 0 else 2]
+            mix, low = ref[e, g, 1], t == 0
+        else:
+            full = 1 if g == 0 else 0
+            if h == near_h and t == full:
+                return ref[e, g, 0 if g == 0 else 1]
+            mix = ref[e, g, 1 if g == 0 else 0]
+            if h == near_h:
+                low = False
+            elif t == full:
+                low = True
+            else:
+                return jnp.zeros((SUBS, LANES), jnp.float32)
+        half = mix[:cut] if low else mix[cut:]
+        none = jnp.zeros((cut, LANES), jnp.float32)
+        return jnp.concatenate([none, half] if up else [half, none], axis=0)
 
     def unpack(e, src):
         sides = ((0, has_left), (1, 1), (2, has_right))
@@ -149,12 +214,12 @@
                             return src[at, cols] if g == 1 else side[e, g // 2, at, cols]
 
                         if s == 0:
-                            value = jnp.where(has(has_below * present), below[e, g, rows, cols], 0.0)
+                            value = jnp.where(has(has_below * present), ghost(below, e, 1, g, h, t), 0.0)
                         else:
                             up = one(count == s - 1) * has_above * present
                             value = jnp.zeros((SUBS, LANES), jnp.float32)
                             if s >= 2:
-                                value = jnp.where(has(up), above[e, g, rows, cols], value)
+                                value = jnp.where(has(up), ghost(above, e, 0, g, h, t), value)
                             if s <= slots:
                                 value = jnp.where(has(one(count >= s) * present), centre(s - 1), value)
                         plane = 1 + s * edge + h * SUBS
@@ -250,10 +315,15 @@
                     yield s, h, t, pl.ds(s * edge + h * SUBS, SUBS), pl.ds(t * LANES, LANES)
 
     source_copy.wait()
-    pick_last(0, source_ref)
-    pl.semaphore_wait(barrier, everyone - 1)
+    pack(0, source_ref)
+    if gossip:
+        near = (1 + one(sfc > 0) + one(sfc < n_sfc - 1)) * (1 + one(grp > 0) + one(grp < n_grp - 1))
+        pl.semaphore_wait(barrier, near - 1)
+    else:
+        pl.semaphore_wait(barrier, everyone - 1)
     start(0, source_ref)
     receive(0, source_ref)
+    greet_far(0, 2)
     unpack(0, source_ref)
     z0 = vcycle()
     for c in range(per_slot, chunks - per_slot):
@@ -275,7 +345,8 @@
         source_out[rows, cols] = source
         acc_rz = acc_rz + source * value
         acc_curv = acc_curv + value * image
-    pick_last(1, image_buf)
+    pack(1, image_buf)
+    hear_far(0, 2)
     start(1, image_buf)
     row = lax.broadcasted_iota(jnp.int32, (1, LANES), 1)
 
@@ -285,6 +356,7 @@
     rz, curv = whole(acc_rz), whole(acc_curv)
     known = jnp.where(row == 0, rz, jnp.where(row == 1, curv, 0.0))
     receive(1, image_buf)
+    greet_far(1, 4)
     unpack(1, image_buf)
 
     def send(slot, peer, device):
@@ -297,6 +369,7 @@
         value = jnp.where(row == 2, whole(acc), known)
         part[...] = value
         red[me] = value
+        hear_far(1, 4)
 
         def go(i, carry):
             peer, device = place(i)
@@ -374,10 +447,10 @@
             vmem((half_padded, LANES), f32),
             vmem(((slots + 2) * SUBS, LANES), f32),
             vmem((slots * SUBS, LANES), f32),
-            vmem((2, edge, width), f32),
+            vmem((2, 2, 5, SUBS, LANES), f32),
             vmem((2, 2, planes, width), f32),
-            vmem((2, 3, edge, width), f32),
-            vmem((2, 3, edge, width), f32),
+            vmem((2, 3, 3, SUBS, LANES), f32),
+            vmem((2, 3, 3, SUBS, LANES), f32),
             vmem((1, LANES), f32),
             vmem((n, 1, LANES), f32),
             dma((2,)),
@@ -385,6 +458,7 @@
             dma((2, len(WAYS))),
             dma((n,)),
             dma((n,)),
+            pltpu.SemaphoreType.REGULAR((2,)),
         ],
         compiler_params=pltpu.CompilerParams(
             collective_id=0, has_side_effects=True, vmem_limit_bytes=16 * 1024 * 1024

time: 29.9 us -> 28.1 us (0.940)
  Pallas kernels: 27.6 us -> 25.8 us
    pallas_call x1, Pallas kernels: 26.8 us -> 25.1 us  [shards(): pl.pallas_call(functools.partial(kernel, (slots, edge, tiles, n_sfc, n_gr...]
where the time goes in v3:
time: 28.1 us; the launch traced here: 28 us
  Pallas kernels  25.8 us (92%)
  between operations  1.29 us (5%)
  local copies, waits for them, and re-layouts  0.83 us (3%)
    pallas_call x1, Pallas kernels, shards(): pl.pallas_call(functools.partial(kernel, (slots, edge, tiles, n_sfc, n_gr...  25.1 us
    unnamed x2, local copies, waits for them, and re-layouts  0.83 us
    pallas_call x1, Pallas kernels, shards(): pl.pallas_call(combine, out_shape=(out, out, out), in_specs=[pl.BlockSpec...  0.72 us

profile of v3, /device:TPU:0, one launch (start us, length us, event | category | flops | bytes accessed | tf_op | source)
XLA Modules:
  0.0 28.0 jit_solution(15638111848480014852)
XLA Ops:
  1.3 0.0 copy-start
  1.3 0.8 %copy-done = f32[4,16,256]{2,1,0:T(8,128)S(1)} copy-done((f32[4,16,256]{2,1,0:T(8,128)S(1)}, f32[4,16,256]{2,1,0:T(8,128)}, u32[]{:S(2)}) %copy-start) | copy-done | bytes 65560
  2.1 25.1 %pcg.1 = (f32[64,256]{1,0:T(8,128)S(1)}, f32[64,256]{1,0:T(8,128)S(1)}, f32[64,256]{1,0:T(8,128)S(1)}, f32[64,256]{1,0:T(8,128)S(1)}, f32[2,128]{1,0:T(2,128)S(1)}) custom-call(s32[1]{0:T(128)S(6)} %copy.5.count_hbm, f32[64,256]{1,0:T(8,128)S(1)} %bitcast.4), custom_call_target="tpu_custom_call" | custom-call | tf_op jit(solution)/shard_map/pcg/pallas_call | solution.py:433
  27.2 0.7 %combine.1 = (f32[64,256]{1,0:T(8,128)}, f32[64,256]{1,0:T(8,128)}, f32[64,256]{1,0:T(8,128)}) custom-call(f32[64,256]{1,0:T(8,128)S(1)} %get-tuple-element.11.first, f32[64,256]{1,0:T(8,128)S(1)} %get-tuple-element.12.image, f32[64,256]{1,0:T(8,128)S(1)} %get-tuple-element.13.w, f32[64,256]{1,0:T(8,128)S(1)} %get-tuple-element.14.source, ...), custom_call_target="tpu_custom_call" | custom-call | tf_op jit(solution)/shard_map/combine/pallas_call | solution.py:468
Async XLA Ops:
  1.3 0.8 %copy-start = (f32[4,16,256]{2,1,0:T(8,128)S(1)}, f32[4,16,256]{2,1,0:T(8,128)}, u32[]{:S(2)}) copy-start(f32[4,16,256]{2,1,0:T(8,128)} %param.2) | copy-start | bytes 196612
